TPU v7x, 32 devices: a whole 2x2x4 slice. The times are simulated.
32 devices in a mesh: data: 2 (over x), hid: 4 (over z), vocab: 4 (over y, core).
Axes of the slice: x: 2, y: 2, z: 4, core: 2. Of those that a mesh axis runs over, the one named last changes fastest.
Arguments:
- h_states: bfloat16 [2048, 2048], P('data', 'hid'), parts along dimension 0
- w_head: bfloat16 [2048, 100352], P('hid', 'vocab')
- inv_temp: float32 [2048], P('data'), parts along dimension 0
- tgt_ids: int32 [2048], P('data'), parts along dimension 0
Outputs:
- output 1: float32 [2048, 100352], P('data', ('vocab', 'hid')), parts along dimension 0
- output 2: float32 [2048], P('data'), parts along dimension 0
There are 2 independent parts. A program takes and returns all parts, laid end to end along the dimension named above; an argument that names none is the same for every part.
All inputs are finite; a program needn't handle non-finite values.
Results may differ from a plain program's by a relative error of at most 0.001.
Values are sent between devices in bfloat16 or wider.
A program may use at most 1 GiB of HBM per device.

v0:
```python
import jax
import jax.numpy as jnp
from jax import lax
from jax.sharding import PartitionSpec as P


def solution(mesh):
    hid_size = mesh.shape["hid"]
    voc_size = mesh.shape["vocab"]

    def local_step(h_blk, w_blk, temp_blk, tgt_blk):
        part_logits = jnp.dot(h_blk, w_blk, preferred_element_type=jnp.float32)
        logits = lax.psum_scatter(part_logits, "hid", scatter_dimension=1, tiled=True) * temp_blk[:, None]
        local_cols = logits.shape[1]
        glob_max = lax.pmax(jnp.max(logits, axis=1), ("vocab", "hid"))
        exp_vals = jnp.exp(logits - glob_max[:, None])
        glob_sum = lax.psum(jnp.sum(exp_vals, axis=1), ("vocab", "hid"))
        local_cdf = jnp.cumsum(exp_vals / glob_sum[:, None], axis=1)
        hid_tots = lax.all_gather(local_cdf[:, -1], "hid")
        vocab_tots = lax.all_gather(jnp.sum(hid_tots, axis=0), "vocab")
        hid_idx = lax.axis_index("hid")
        voc_idx = lax.axis_index("vocab")
        hid_off = jnp.sum(jnp.where((jnp.arange(hid_size) < hid_idx)[:, None], hid_tots, 0.0), axis=0)
        voc_off = jnp.sum(jnp.where((jnp.arange(voc_size) < voc_idx)[:, None], vocab_tots, 0.0), axis=0)
        cdf_blk = local_cdf + (voc_off + hid_off)[:, None]
        col_start = (voc_idx * hid_size + hid_idx) * local_cols
        local_pos = tgt_blk - col_start
        in_range = (local_pos >= 0) & (local_pos < local_cols)
        picked = jnp.take_along_axis(cdf_blk, jnp.clip(local_pos, 0, local_cols - 1)[:, None], axis=1)[:, 0]
        cdf_tgt = lax.psum(jnp.where(in_range, picked, 0.0), ("vocab", "hid"))
        return cdf_blk, cdf_tgt

    return jax.shard_map(local_step, mesh=mesh, in_specs=(P("data", "hid"), P("hid", "vocab"), P("data"), P("data")), out_specs=(P("data", ("vocab", "hid")), P("data")), check_vma=False)
```

profile of v0, /device:TPU:0, one launch (start us, length us, event | category | flops | bytes accessed | tf_op | source)
XLA Modules:
  0.0 2036.9 jit_solution(1278084352248921839)
XLA Ops:
  7.2 0.0 copy-start
  7.2 0.0 reduce-scatter.2.cloned.1.call-start
  7.2 1.2 copy-done
  8.4 45.0 %fusion.7 = f32[1024,25088]{1,0:T(8,128)} fusion(bf16[1024,512]{1,0:T(8,128)(2,1)S(1)} %copy-done, bf16[512,25088]{1,0:T(8,128)(2,1)} %param.5), kind=kOutput, calls=%fused_computation.22 | convolution fusion | flops 26306674688 | bytes 129499136 | tf_op jit(solution)/shard_map/dot_general | solution.py:12
  53.4 0.0 reduce-scatter.2.cloned.1.call-update
  53.5 0.6 copy-done.3
  54.2 1663.9 %reduce-scatter.2.cloned.1.call-done = f32[1024,6272]{1,0:T(8,128)} async-done(((f32[1024,25088]{1,0:T(8,128)}), f32[1024,6272]{1,0:T(8,128)}) %reduce-scatter.2.cloned.1.call-update) | async-done | bytes 25690128 | tf_op jit(solution)/shard_map/reduce_scatter | solution.py:13
  1718.1 0.0 copy-done.2
  1718.1 10.5 multiply_reduce_fusion
  1728.6 31.9 %pmax.7 = f32[1024]{0:T(1024)S(1)} all-reduce(f32[1024]{0:T(1024)S(1)} %multiply_reduce_fusion), channel_id=1, replica_groups=mesh['data'=2,'hid'=4,'vocab'=4] {'vocab','hid'}, use_global_device_ids=true, to_apply=%region_2.0 | all-reduce | flops 1024 | bytes 8192 | tf_op jit(solution)/shard_map/pmax | solution.py:15
  1760.5 11.8 fusion.3
  1772.4 29.9 %psum.14 = f32[1024]{0:T(1024)S(1)} all-reduce(f32[1024]{0:T(1024)S(1)} %fusion.3), channel_id=1, replica_groups=mesh['data'=2,'hid'=4,'vocab'=4] {'vocab','hid'}, use_global_device_ids=true, to_apply=%region_4.0 | all-reduce | flops 1024 | bytes 8192 | tf_op jit(solution)/shard_map/psum | solution.py:17
  1802.2 19.1 fusion.2
  1821.3 25.8 %copy.11 = f32[1024,6272]{0,1:T(8,128)} copy(f32[1024,6272]{1,0:T(8,128)} %fusion.2) | data formatting | bytes 51380224 | tf_op jit(solution)/shard_map/div | solution.py:18
  1847.1 26.5 %fusion = f32[1024,49,128]{0,1,2:T(8,128)} fusion(f32[1024,49,128]{0,2,1:T(8,128)} %bitcast.14), kind=kOutput, calls=%fused_computation.1 | output fusion | flops 815661056 | bytes 51380224 | tf_op jit(solution)/shard_map/reduce-window
  1873.6 1.0 slice_bitcast_fusion
  1874.6 0.2 reduce-window.9
  1874.8 11.2 broadcast_add_fusion
  1886.0 30.5 %copy.13 = f32[1024,49,128]{0,2,1:T(8,128)} copy(f32[1024,49,128]{0,1,2:T(8,128)S(1)} %broadcast_add_fusion) | data formatting | bytes 51380224 | tf_op jit(solution)/shard_map/reduce_window_sum
  1916.5 0.8 slice.16
  1917.3 25.8 %copy.14 = f32[1024,6272]{1,0:T(8,128)} copy(f32[1024,6272]{0,1:T(8,128)} %bitcast.13) | data formatting | bytes 51380224 | tf_op jit(solution)/shard_map/reduce_window_sum
  1943.1 13.0 all-gather
  1956.1 0.5 broadcast.52
  1956.6 0.7 reduce.3
  1957.3 0.1 select_reduce_fusion
  1957.4 5.2 all-gather.1
  1962.6 0.1 select_reduce_fusion.1
  1962.7 0.0 copy-start.1
  1962.7 17.8 broadcast_add_fusion.1
  1980.5 17.1 gather_fusion
  1997.6 32.4 %psum.15 = f32[1024]{0:T(1024)} all-reduce(f32[1024]{0:T(1024)S(1)} %select_select_fusion), channel_id=1, replica_groups=mesh['data'=2,'hid'=4,'vocab'=4] {'vocab','hid'}, use_global_device_ids=true, to_apply=%region_10.11 | all-reduce | flops 1024 | bytes 8192 | tf_op jit(solution)/shard_map/psum | solution.py:30
  2030.0 0.0 copy-done.1
  (12 shorter events, 0.1 us)
Async XLA Ops:
  7.2 1.2 copy-start
  7.2 1710.9 %reduce-scatter.2.cloned.1.call-start = ((), (), s32[]{:S(2)}) async-start(), calls=%async_computation.1 | async-start | bytes 128450560 | tf_op jit(solution)/shard_map/reduce_scatter | solution.py:13
  53.4 0.7 copy-start.3
  53.4 1664.7 %copy-start.2 = (f32[1024]{0:T(1024)S(1)}, f32[1024]{0:T(1024)}, u32[]{:S(2)}) copy-start(f32[1024]{0:T(1024)} %param.6) | copy-start | bytes 12292
  1962.7 67.3 %copy-start.1 = (bf16[1024,512]{1,0:T(8,128)(2,1)S(1)}, bf16[1024,512]{1,0:T(8,128)(2,1)}, u32[]{:S(2)}) copy-start(bf16[1024,512]{1,0:T(8,128)(2,1)} %param.4) | copy-start | bytes 3145732
Sparse Core Ops, SparseCore 0:
  53.6 1664.4 reduce-scatter.1
where the time goes:
time: 2040 us
  waiting for transfers between devices  1660 us (81%)
  blocking collectives  112 us (5%)
  local copies, waits for them, and re-layouts  103 us (5%)
  other arithmetic  98.1 us (5%)
  matrix products  45 us (2%)
    reduce_scatter x1, waiting for transfers between devices, local_step(): lax.psum_scatter(part_logits, 'hid', scatter_dimension=1, tiled=True)  1660 us
    another operation x3, local copies, waits for them, and re-layouts  57.3 us
    dot_general x1, matrix products, local_step(): part_logits = jnp.dot(h_blk, w_blk, preferred_element_type=jnp.float32)  45 us
  transfers between devices with their start and end apart: 1, of which 1 were waited for; matrix products, arithmetic and copies ran while one was open for 0% of the time, Pallas kernels for 0%

commit v1 on v0

v1 whole, which is shorter than its diff:
```python
import functools

import jax
import jax.numpy as jnp
from jax import lax
from jax.experimental import pallas as pl
from jax.experimental.pallas import tpu as pltpu
from jax.sharding import PartitionSpec as P

MESH = pl.DeviceIdType.MESH
F32 = jnp.float32
BF16 = jnp.bfloat16
TILE = 256
LANES = 128
LOWEST = float(jnp.finfo(jnp.float32).min)


def chunks_of(tiles):
    sizes, left = [], tiles
    for size in (1, 1, 2, 2, 3):
        if left > size:
            sizes.append(size)
            left -= size
    while left > 0:
        sizes.append(min(4, left))
        left -= sizes[-1]
    starts, at = [], 0
    for size in reversed(sizes):
        starts.append((at, size))
        at += size
    return starts


def split3(e):
    hi = e.astype(BF16)
    rest = e - hi.astype(F32)
    mid = rest.astype(BF16)
    low = (rest - mid.astype(F32)).astype(BF16)
    return hi, mid, low


def prefix_kernel(
    n_cols, h_ref, w_ref, temp_ref, tgt_ref,
    c_ref, scale_ref, off_ref, tgt_out_ref,
    wbuf, hbuf, tri, tri_last, m_all, s_all, t_all, temp_col, rel_col, zmsg, vmsg, back,
    ws, wr, xs, xr, wl, hl, hs, hr, zs, zr, vs, vr,
):
    x, z, v = lax.axis_index("data"), lax.axis_index("hid"), lax.axis_index("vocab")
    rows, depth = h_ref.shape
    half, quarter = depth // 2, rows // 4
    n_tiles = pl.cdiv(n_cols, TILE)
    last_width = n_cols - (n_tiles - 1) * TILE
    plan = chunks_of(n_tiles)
    n_chunks = len(plan)

    side = z // 2
    outer_far, inner_far, near = 3 - 3 * side, 2 - side, 1 - z + 4 * side
    is_outer = jnp.where(z == side * 3, 1, 0)
    z_two, z_one = lax.rem(z + 2, 4), near
    v_two, v_one = lax.rem(v + 2, 4), v + 1 - 2 * lax.rem(v, 2)
    sources = (near, inner_far, outer_far)

    def cols_of(j):
        first, size = plan[j]
        start = first * TILE
        return start, min(n_cols, (first + size) * TILE) - start

    def w_rows(source, part):
        return pl.ds(pl.multiple_of(source * depth + part * half, half), half)

    def w_place(j, source, part):
        start, n = cols_of(j)
        return wbuf.at[w_rows(source, part), pl.ds(start, n)]

    def h_place(q, block=None):
        at = pl.ds(pl.multiple_of(q * quarter, quarter), quarter)
        if block is None:
            return hbuf.at[at]
        return hbuf.at[at, pl.ds(pl.multiple_of(block * depth, depth), depth)]

    def remote(src, dst, send, recv, **to):
        return pltpu.make_async_remote_copy(
            src_ref=src, dst_ref=dst, send_sem=send, recv_sem=recv, device_id=to, device_id_type=MESH
        )

    def direct(j, k, dest, slot):
        start, n = cols_of(j)
        src = w_ref.at[
            pl.ds(pl.multiple_of(x * half, half), half),
            pl.ds(pl.multiple_of(dest * n_cols + start, LANES), n),
        ]
        return remote(src, w_place(j, z, x), ws.at[j, k], wr.at[j, slot], hid=dest)

    def send_near(j):
        return direct(j, 0, near, 0)

    def send_inner(j):
        return direct(j, 1, inner_far, 1 + is_outer)

    def send_outer(j):
        return direct(j, 2, outer_far, 1 + is_outer)

    def landed(j, k):
        place = w_place(j, sources[k], x)
        remote(place, place, ws.at[j, k], wr.at[j, k], hid=sources[k]).wait_recv()

    def forward(j, k):
        place = w_place(j, sources[k], x)
        return remote(place, place, xs.at[j, k], xr.at[j, k], data=1 - x)

    def forwarded(j, k):
        place = w_place(j, sources[k], 1 - x)
        remote(place, place, xs.at[j, k], xr.at[j, k], data=1 - x).wait_recv()

    def own(j):
        start, n = cols_of(j)
        return pltpu.make_async_copy(
            w_ref.at[:, pl.ds(pl.multiple_of(z * n_cols + start, LANES), n)],
            wbuf.at[pl.ds(pl.multiple_of(z * depth, depth), depth), pl.ds(start, n)],
            wl.at[j],
        )

    h_mine = h_ref.at[pl.ds(pl.multiple_of(v * quarter, quarter), quarter)]
    h_own = pltpu.make_async_copy(h_mine, h_place(v, z), hl)
    h_two = remote(h_mine, h_place(v, z), hs.at[0], hr.at[0], hid=z_two)
    h_one = remote(h_mine, h_place(v, z), hs.at[1], hr.at[1], hid=z_one)
    h_relay = remote(h_place(v, z_two), h_place(v, z_two), hs.at[2], hr.at[2], hid=z_one)
    h_chip = remote(h_place(v), h_place(v), hs.at[3], hr.at[3], vocab=v_two)
    h_core = remote(h_place(v), h_place(v), hs.at[4], hr.at[4], vocab=v_one)
    h_both = remote(h_place(v_two), h_place(v_two), hs.at[5], hr.at[5], vocab=v_one)

    def arrived(place, i, **frm):
        remote(place, place, hs.at[i], hr.at[i], **frm).wait_recv()

    barrier = pltpu.get_barrier_semaphore()
    peers = [{"hid": lax.rem(z + d, 4)} for d in (1, 2, 3)]
    peers += [{"data": 1 - x}] + [{"vocab": lax.rem(v + d, 4)} for d in (1, 2, 3)]
    for peer in peers:
        pl.semaphore_signal(barrier, inc=1, device_id=peer, device_id_type=MESH)
    h_own.start()
    own(0).start()
    pl.semaphore_wait(barrier, len(peers))

    h_two.start()
    h_one.start()
    send_near(0).start()
    send_outer(0).start()

    def ones_below(ref, width):
        k = lax.broadcasted_iota(jnp.int32, (width, width), 0)
        c = lax.broadcasted_iota(jnp.int32, (width, width), 1)
        block = jnp.where(k <= c, 1.0, 0.0).astype(BF16)
        for i in range(3):
            ref[pl.ds(i * width, width), :] = block

    ones_below(tri, TILE)
    if last_width != TILE:
        ones_below(tri_last, last_width)
    base = (v * 4 + z) * n_cols
    back[0:1, :] = temp_ref[...]
    back[1:2, :] = (tgt_ref[...] - base).astype(F32)
    cols8 = back[...].T
    temp_col[...] = cols8[:, 0:1]
    rel_col[...] = cols8[:, 1:2].astype(jnp.int32)
    m_all[...] = jnp.full(m_all.shape, LOWEST, F32)
    s_all[...] = jnp.zeros(s_all.shape, F32)
    t_all[...] = jnp.zeros(t_all.shape, F32)

    arrived(h_place(v, z_two), 0, hid=z_two)
    h_relay.start()
    near_at = 1
    for j in range(n_chunks):
        while near_at < min(n_chunks, 3 + 2 * j):
            send_near(near_at).start()
            near_at += 1
        if j > 0:
            send_outer(j).start()
        send_inner(j).start()
    if n_chunks > 1:
        own(1).start()
    arrived(h_place(v, z_one), 1, hid=z_one)
    far = lax.rem(z_one + 2, 4)
    arrived(h_place(v, far), 2, hid=z_one)
    h_own.wait()
    h_chip.start()
    h_core.start()
    landed(0, 0)
    forward(0, 0).start()
    arrived(h_place(v_two), 3, vocab=v_two)
    h_both.start()

    def tile(t, start, width, table):
        span = pl.ds(start, width)
        part = min(rows, 512)

        @pl.loop(0, rows // part)
        def _(i):
            at = pl.ds(pl.multiple_of(i * part, part), part)
            c_ref[at, span] = jnp.dot(hbuf[at, :], wbuf[:, span], preferred_element_type=F32)

        few = min(rows, 256)

        @pl.loop(0, rows // few)
        def _(i):
            at = pl.ds(pl.multiple_of(i * few, few), few)
            logits = c_ref[at, span] * temp_col[at, :]
            top = jnp.max(logits, axis=1, keepdims=True)
            e = jnp.exp(logits - top)
            sums = jnp.dot(jnp.concatenate(split3(e), axis=1), table[...], preferred_element_type=F32)
            c_ref[at, span] = sums
            lane = lax.broadcasted_iota(jnp.int32, (few, width), 1)
            hit = jnp.where(lane == rel_col[at, :] - start, sums, 0.0)
            here = lax.broadcasted_iota(jnp.int32, (few, LANES), 1) == t
            m_all[at, :] = jnp.where(here, top, m_all[at, :])
            s_all[at, :] = jnp.where(here, sums[:, width - 1 : width], s_all[at, :])
            t_all[at, :] = jnp.where(here, jnp.sum(hit, axis=1, keepdims=True), t_all[at, :])

    def compute(j):
        first, size = plan[j]
        whole = size if first + size < n_tiles or last_width == TILE else size - 1
        if whole:

            @pl.loop(first, first + whole)
            def _(t):
                tile(t, pl.multiple_of(t * TILE, TILE), TILE, tri)

        if whole < size:
            tile(n_tiles - 1, (n_tiles - 1) * TILE, last_width, tri_last)

    def complete(j):
        for k in range(3):
            forwarded(j, k)
        own(j).wait()

    near_at = 1
    for j in range(n_chunks):
        while near_at < min(n_chunks, 2 + 2 * j):
            landed(near_at, 0)
            forward(near_at, 0).start()
            near_at += 1
        for k in (1, 2):
            landed(j, k)
            forward(j, k).start()
        if j == 0:
            arrived(h_place(v_one), 4, vocab=v_one)
            arrived(h_place(lax.rem(v_one + 2, 4)), 5, vocab=v_one)
        else:
            complete(j - 1)
            compute(j - 1)
        if j + 2 < n_chunks:
            own(j + 2).start()
    complete(n_chunks - 1)
    compute(n_chunks - 1)

    lane = lax.broadcasted_iota(jnp.int32, (rows, LANES), 1)
    top = jnp.max(m_all[...], axis=1, keepdims=True)
    shrink = jnp.exp(m_all[...] - top)
    parts = s_all[...] * shrink
    k = lax.broadcasted_iota(jnp.int32, (LANES, LANES), 0)
    c = lax.broadcasted_iota(jnp.int32, (LANES, LANES), 1)
    strict = jnp.where(k < c, 1.0, 0.0).astype(BF16)
    before = sum(jnp.dot(p, strict, preferred_element_type=F32) for p in split3(parts))
    s_all[...] = before
    rel = rel_col[...]
    holds = (rel >= lane * TILE) & (rel < (lane + 1) * TILE) & (rel < n_cols)
    found = t_all[...] * shrink + jnp.where(holds, before, 0.0)
    total = jnp.sum(parts, axis=1, keepdims=True)
    at_tgt = jnp.sum(found, axis=1, keepdims=True)
    packed = jnp.where(lane == 0, top, jnp.where(lane == 1, total, at_tgt))
    zmsg[z] = packed.T[0:4, :]

    for j in range(n_chunks):
        send_near(j).wait_send()
        send_inner(j).wait_send()
        send_outer(j).wait_send()
        for k in range(3):
            forward(j, k).wait_send()
    for copy in (h_two, h_one, h_relay, h_chip, h_core, h_both):
        copy.wait_send()

    def z_send(d):
        to = lax.rem(z + d, 4)
        return remote(zmsg.at[z], zmsg.at[z], zs.at[d - 1], zr.at[d - 1], hid=to)

    def v_send(d):
        to = lax.rem(v + d, 4)
        return remote(vmsg.at[v], vmsg.at[v], vs.at[d - 1], vr.at[d - 1], vocab=to)

    for d in (1, 2, 3):
        z_send(d).start()
    for d in (1, 2, 3):
        frm = lax.rem(z + 4 - d, 4)
        remote(zmsg.at[frm], zmsg.at[frm], zs.at[d - 1], zr.at[d - 1], hid=frm).wait_recv()

    ids = tgt_ref[...]
    maxes = [zmsg[h, 0:1, :] for h in range(4)]
    v_max = functools.reduce(jnp.maximum, maxes)
    v_sum = jnp.zeros((1, rows), F32)
    v_tgt = jnp.zeros((1, rows), F32)
    mine_before = jnp.zeros((1, rows), F32)
    for h in range(4):
        mine_before = jnp.where(h == z, v_sum, mine_before)
        f = jnp.exp(maxes[h] - v_max)
        low = (v * 4 + h) * n_cols
        inside = (ids >= low) & (ids < low + n_cols)
        v_tgt += jnp.where(inside, zmsg[h, 2:3, :] * f + v_sum, 0.0)
        v_sum += zmsg[h, 1:2, :] * f
    vmsg[v, 0:1, :] = v_max
    vmsg[v, 1:2, :] = v_sum
    vmsg[v, 2:3, :] = v_tgt
    vmsg[v, 3:4, :] = v_tgt

    for d in (1, 2, 3):
        z_send(d).wait_send()
    for d in (1, 2, 3):
        v_send(d).start()
    for d in (1, 2, 3):
        frm = lax.rem(v + 4 - d, 4)
        remote(vmsg.at[frm], vmsg.at[frm], vs.at[d - 1], vr.at[d - 1], vocab=frm).wait_recv()

    maxes = [vmsg[u, 0:1, :] for u in range(4)]
    g_max = functools.reduce(jnp.maximum, maxes)
    g_sum = jnp.zeros((1, rows), F32)
    g_tgt = jnp.zeros((1, rows), F32)
    g_before = jnp.zeros((1, rows), F32)
    for u in range(4):
        f = jnp.exp(maxes[u] - g_max)
        g_before = jnp.where(u == v, g_sum + mine_before * f, g_before)
        low = u * 4 * n_cols
        inside = (ids >= low) & (ids < low + 4 * n_cols)
        g_tgt += jnp.where(inside, vmsg[u, 2:3, :] * f + g_sum, 0.0)
        g_sum += vmsg[u, 1:2, :] * f
    tgt_out_ref[...] = g_tgt / g_sum
    back[0:1, :] = g_max
    back[1:2, :] = g_sum
    back[2:3, :] = g_before
    cols8 = back[...].T
    g_max, g_sum, g_before = cols8[:, 0:1], cols8[:, 1:2], cols8[:, 2:3]
    mine = jnp.max(m_all[...], axis=1, keepdims=True)
    scale_ref[...] = jnp.exp(m_all[...] - g_max) / g_sum
    off_ref[...] = (s_all[...] * jnp.exp(mine - g_max) + g_before) / g_sum
    for d in (1, 2, 3):
        v_send(d).wait_send()


def finish_kernel(c_ref, scale_ref, off_ref, tgt_ref, out_ref, tgt_out_ref):
    n, n_cols = out_ref.shape
    at = pl.ds(pl.multiple_of(pl.program_id(0) * n, n), n)
    for start in range(0, n_cols, TILE):
        t, stop = start // TILE, min(n_cols, start + TILE)
        out_ref[:, start:stop] = (
            c_ref[at, start:stop] * scale_ref[at, t : t + 1] + off_ref[at, t : t + 1]
        )
    tgt_out_ref[...] = tgt_ref[...]


def solution(mesh):
    n_hid, n_voc = mesh.shape["hid"], mesh.shape["vocab"]
    assert n_hid == 4 and n_voc == 4 and mesh.shape["data"] == 2

    def local_step(h_blk, w_blk, temp_blk, tgt_blk):
        rows, depth = h_blk.shape
        n_cols = w_blk.shape[1] // n_hid
        n_tiles = pl.cdiv(n_cols, TILE)
        last_width = n_cols - (n_tiles - 1) * TILE
        assert n_tiles <= LANES and n_cols % LANES == 0
        n_chunks = len(chunks_of(n_tiles))
        vmem = pl.BlockSpec(memory_space=pltpu.VMEM)
        hbm = pl.BlockSpec(memory_space=pltpu.HBM)
        dma = pltpu.SemaphoreType.DMA
        table = pltpu.VMEM((rows, LANES), F32)
        c, scale, off, tgt = pl.pallas_call(
            functools.partial(prefix_kernel, n_cols),
            out_shape=(
                pltpu.VMEM((rows, n_cols), F32),
                pltpu.VMEM((rows, LANES), F32),
                pltpu.VMEM((rows, LANES), F32),
                pltpu.VMEM((1, rows), F32),
            ),
            in_specs=[hbm, hbm, vmem, vmem],
            out_specs=[vmem] * 4,
            scratch_shapes=[
                pltpu.VMEM((4 * depth, n_cols), BF16),
                pltpu.VMEM((rows, 4 * depth), BF16),
                pltpu.VMEM((3 * TILE, TILE), BF16),
                pltpu.VMEM((3 * last_width, last_width), BF16),
                table,
                table,
                table,
                pltpu.VMEM((rows, 1), F32),
                pltpu.VMEM((rows, 1), jnp.int32),
                pltpu.VMEM((4, 4, rows), F32),
                pltpu.VMEM((4, 4, rows), F32),
                pltpu.VMEM((8, rows), F32),
                dma((n_chunks, 3)),
                dma((n_chunks, 3)),
                dma((n_chunks, 3)),
                dma((n_chunks, 3)),
                dma((n_chunks,)),
                dma,
                dma((6,)),
                dma((6,)),
                dma((3,)),
                dma((3,)),
                dma((3,)),
                dma((3,)),
            ],
            compiler_params=pltpu.CompilerParams(
                collective_id=0, has_side_effects=True, vmem_limit_bytes=37 << 20
            ),
            name="prefix",
        )(h_blk, w_blk, temp_blk.reshape(1, rows), tgt_blk.reshape(1, rows))
        n = min(rows, 128)
        cdf, cdf_tgt = pl.pallas_call(
            finish_kernel,
            grid=(rows // n,),
            out_shape=(
                jax.ShapeDtypeStruct((rows, n_cols), F32),
                jax.ShapeDtypeStruct((1, rows), F32),
            ),
            in_specs=[vmem] * 4,
            out_specs=[
                pl.BlockSpec((n, n_cols), lambda i: (i, 0)),
                pl.BlockSpec((1, rows), lambda i: (0, 0)),
            ],
            compiler_params=pltpu.CompilerParams(vmem_limit_bytes=9 << 20),
            name="finish",
        )(c, scale, off, tgt)
        return cdf, cdf_tgt.reshape(rows)

    return jax.shard_map(
        local_step,
        mesh=mesh,
        in_specs=(P("data", "hid"), P("hid", "vocab"), P("data"), P("data")),
        out_specs=(P("data", ("vocab", "hid")), P("data")),
        check_vma=False,
    )
```

time: 2040 us -> 353 us (0.17)
  waiting for transfers between devices: 1660 us -> 0 us
  Pallas kernels: 0 us -> 352 us
  blocking collectives: 112 us -> 0 us
  local copies, waits for them, and re-layouts: 103 us -> 0 us
  other arithmetic: 98.1 us -> 0 us
  matrix products: 45 us -> 0 us
    reduce_scatter x1 -> x0, waiting for transfers between devices: 1660 us -> none  [local_step(): lax.psum_scatter(part_logits, 'hid', scatter_dimension=1, tiled=True)]
    pallas_call x0 -> x2, Pallas kernels: none -> 352 us  [the longest x1 341 us: local_step(): pl.pallas_call(functools.partial(prefix_kernel, n_cols), out_shape=(pltpu...]
    psum x2 -> x0, blocking collectives: 62.2 us -> none  [the longest x1 32.4 us: local_step(): cdf_tgt = lax.psum(jnp.where(in_range, picked, 0.0), ('vocab', 'hid'))]
    another operation x3 -> x0, local copies, waits for them, and re-layouts: 57.3 us -> none
    dot_general x1 -> x0, matrix products: 45 us -> none  [local_step(): part_logits = jnp.dot(h_blk, w_blk, preferred_element_type=jnp.float32)]
    another operation x3 -> x0, other arithmetic: 38 us -> none
    pmax x1 -> x0, blocking collectives: 31.9 us -> none  [local_step(): glob_max = lax.pmax(jnp.max(logits, axis=1), ('vocab', 'hid'))]
    div x1 -> x0, local copies, waits for them, and re-layouts: 25.8 us -> none  [local_step(): local_cdf = jnp.cumsum(exp_vals / glob_sum[:, None], axis=1)]
  transfers between devices with their start and end apart: 1 -> 0, of which waited for: 1 -> 0; matrix products, arithmetic and copies ran while one was open for 0% -> 0% of each run, Pallas kernels for 0% -> 0%
where the time goes in v1:
time: 353 us
  Pallas kernels  352 us (100%)
    pallas_call x1, Pallas kernels, local_step(): pl.pallas_call(functools.partial(prefix_kernel, n_cols), out_shape=(pltpu...  341 us
    pallas_call x1, Pallas kernels, local_step(): pl.pallas_call(finish_kernel, grid=(rows // n,), out_shape=(jax.ShapeDtyp...  11.6 us

profile of v1, /device:TPU:0, one launch (start us, length us, event | category | flops | bytes accessed | tf_op | source)
XLA Modules:
  0.0 352.8 jit_solution(10074032484635456134)
XLA Ops:
  0.6 340.6 %prefix.1 = (f32[1024,6272]{1,0:T(8,128)S(1)}, f32[1024,128]{1,0:T(8,128)S(1)}, f32[1024,128]{1,0:T(8,128)S(1)}, f32[1,1024]{1,0:T(1,128)S(1)}) custom-call(bf16[1024,512]{1,0:T(8,128)(2,1)} %h_ref.1, bf16[512,25088]{1,0:T(8,128)(2,1)} %w_ref.1, f32[1,1024]{1,0:T(1,128)} %bitcast.3, s32[1,1024]{1,0:T(1,128)} %bitcast.4), custom_call_target="tpu_custom_call" | custom-call | tf_op jit(solution)/shard_map/prefix/pallas_call | solution.py:372
  341.2 11.6 %finish.1 = (f32[1024,6272]{1,0:T(8,128)}, f32[1,1024]{1,0:T(1,128)}) custom-call(f32[1024,6272]{1,0:T(8,128)S(1)} %get-tuple-element.8.c_ref, f32[1024,128]{1,0:T(8,128)S(1)} %get-tuple-element.9.scale_ref, f32[1024,128]{1,0:T(8,128)S(1)} %get-tuple-element.10.off_ref, f32[1,1024]{1,0:T(1,128)S(1)} %get-tuple-element.11.tgt_ref), custom_call_target="tpu_custom_call" | custom-call | tf_op jit(solution)/shard_map/finish/pallas_call | solution.py:414

commit v2 on v1

--- a/solution.py
+++ b/solution.py
@@ -94,11 +94,15 @@
     def send_near(j):
         return direct(j, 0, near, 0)
 
+    odd = lax.rem(v, 2)
+    far_first = outer_far + odd * (inner_far - outer_far)
+    far_second = inner_far + odd * (outer_far - inner_far)
+
     def send_inner(j):
-        return direct(j, 1, inner_far, 1 + is_outer)
+        return direct(j, 1, far_second, 1 + is_outer)
 
     def send_outer(j):
-        return direct(j, 2, outer_far, 1 + is_outer)
+        return direct(j, 2, far_first, 1 + is_outer)
 
     def landed(j, k):
         place = w_place(j, sources[k], x)

time: 353 us -> 345 us (0.977)
  Pallas kernels: 352 us -> 344 us
    pallas_call x1, Pallas kernels: 341 us -> 333 us  [local_step(): pl.pallas_call(functools.partial(prefix_kernel, n_cols), out_shape=(pltpu...]
where the time goes in v2:
time: 345 us
  Pallas kernels  344 us (100%)
    pallas_call x1, Pallas kernels, local_step(): pl.pallas_call(functools.partial(prefix_kernel, n_cols), out_shape=(pltpu...  333 us
    pallas_call x1, Pallas kernels, local_step(): pl.pallas_call(finish_kernel, grid=(rows // n,), out_shape=(jax.ShapeDtyp...  11.6 us

profile of v2, /device:TPU:0, one launch (start us, length us, event | category | flops | bytes accessed | tf_op | source)
XLA Modules:
  0.0 345.0 jit_solution(2182358351301638632)
XLA Ops:
  0.6 332.8 %prefix.1 = (f32[1024,6272]{1,0:T(8,128)S(1)}, f32[1024,128]{1,0:T(8,128)S(1)}, f32[1024,128]{1,0:T(8,128)S(1)}, f32[1,1024]{1,0:T(1,128)S(1)}) custom-call(bf16[1024,512]{1,0:T(8,128)(2,1)} %h_ref.1, bf16[512,25088]{1,0:T(8,128)(2,1)} %w_ref.1, f32[1,1024]{1,0:T(1,128)} %bitcast.3, s32[1,1024]{1,0:T(1,128)} %bitcast.4), custom_call_target="tpu_custom_call" | custom-call | tf_op jit(solution)/shard_map/prefix/pallas_call | solution.py:376
  333.4 11.6 %finish.1 = (f32[1024,6272]{1,0:T(8,128)}, f32[1,1024]{1,0:T(1,128)}) custom-call(f32[1024,6272]{1,0:T(8,128)S(1)} %get-tuple-element.8.c_ref, f32[1024,128]{1,0:T(8,128)S(1)} %get-tuple-element.9.scale_ref, f32[1024,128]{1,0:T(8,128)S(1)} %get-tuple-element.10.off_ref, f32[1,1024]{1,0:T(1,128)S(1)} %get-tuple-element.11.tgt_ref), custom_call_target="tpu_custom_call" | custom-call | tf_op jit(solution)/shard_map/finish/pallas_call | solution.py:418

commit v3 on v1

--- a/solution.py
+++ b/solution.py
@@ -17,12 +17,12 @@
 
 def chunks_of(tiles):
     sizes, left = [], tiles
-    for size in (1, 1, 2, 2, 3):
+    for size in (1, 1, 1, 2, 2):
         if left > size:
             sizes.append(size)
             left -= size
     while left > 0:
-        sizes.append(min(4, left))
+        sizes.append(min(3, left))
         left -= sizes[-1]
     starts, at = [], 0
     for size in reversed(sizes):
@@ -31,6 +31,18 @@
     return starts
 
 
+def service_order(plan, tiles):
+    half = tiles / 2
+    events = [(0.5 * tiles, "h line", 0), (0.9 * tiles, "h chip", 0)]
+    for j, (first, size) in enumerate(plan):
+        end = first + size
+        events.append((end, 0, j))
+        events.append((2 * end if end < half else tiles + 4 * (end - half), 1, j))
+        events.append((tiles + 4 * end if end < half else 3 * tiles + 2 * (end - half), 2, j))
+    events.sort(key=lambda e: e[0])
+    return [e[1:] for e in events]
+
+
 def split3(e):
     hi = e.astype(BF16)
     rest = e - hi.astype(F32)
@@ -41,9 +53,9 @@
 
 def prefix_kernel(
     n_cols, h_ref, w_ref, temp_ref, tgt_ref,
-    c_ref, scale_ref, off_ref, tgt_out_ref,
+    c_ref, scale_ref, off_ref, tgt_out_ref, relay_ref,
     wbuf, hbuf, tri, tri_last, m_all, s_all, t_all, temp_col, rel_col, zmsg, vmsg, back,
-    ws, wr, xs, xr, wl, hl, hs, hr, zs, zr, vs, vr,
+    ws, wr, xs, xr, rs, rr, wl, hl, hs, hr, zs, zr, vs, vr,
 ):
     x, z, v = lax.axis_index("data"), lax.axis_index("hid"), lax.axis_index("vocab")
     rows, depth = h_ref.shape
@@ -97,8 +109,24 @@
     def send_inner(j):
         return direct(j, 1, inner_far, 1 + is_outer)
 
+    def relay_place(j, s):
+        start, n = cols_of(j)
+        return relay_ref.at[s, :, pl.ds(start, n)]
+
     def send_outer(j):
-        return direct(j, 2, outer_far, 1 + is_outer)
+        start, n = cols_of(j)
+        src = w_ref.at[
+            pl.ds(pl.multiple_of(x * half, half), half),
+            pl.ds(pl.multiple_of(outer_far * n_cols + start, LANES), n),
+        ]
+        return remote(src, relay_place(j, is_outer), ws.at[j, 2], rr.at[j, is_outer], hid=inner_far)
+
+    def relay_landed(j, s):
+        place = relay_place(j, s)
+        remote(place, place, ws.at[j, 2], rr.at[j, s], hid=inner_far).wait_recv()
+
+    def relay(j, s):
+        return remote(relay_place(j, s), w_place(j, sources[1 + s], x), rs.at[j, s], wr.at[j, 1 + s], hid=near)
 
     def landed(j, k):
         place = w_place(j, sources[k], x)
@@ -168,26 +196,14 @@
 
     arrived(h_place(v, z_two), 0, hid=z_two)
     h_relay.start()
-    near_at = 1
-    for j in range(n_chunks):
-        while near_at < min(n_chunks, 3 + 2 * j):
-            send_near(near_at).start()
-            near_at += 1
-        if j > 0:
-            send_outer(j).start()
+    for j in range(1, n_chunks):
+        send_near(j).start()
+    send_inner(0).start()
+    for j in range(1, n_chunks):
+        send_outer(j).start()
         send_inner(j).start()
     if n_chunks > 1:
         own(1).start()
-    arrived(h_place(v, z_one), 1, hid=z_one)
-    far = lax.rem(z_one + 2, 4)
-    arrived(h_place(v, far), 2, hid=z_one)
-    h_own.wait()
-    h_chip.start()
-    h_core.start()
-    landed(0, 0)
-    forward(0, 0).start()
-    arrived(h_place(v_two), 3, vocab=v_two)
-    h_both.start()
 
     def tile(t, start, width, table):
         span = pl.ds(start, width)
@@ -232,23 +248,37 @@
             forwarded(j, k)
         own(j).wait()
 
-    near_at = 1
-    for j in range(n_chunks):
-        while near_at < min(n_chunks, 2 + 2 * j):
-            landed(near_at, 0)
-            forward(near_at, 0).start()
-            near_at += 1
-        for k in (1, 2):
-            landed(j, k)
-            forward(j, k).start()
-        if j == 0:
-            arrived(h_place(v_one), 4, vocab=v_one)
-            arrived(h_place(lax.rem(v_one + 2, 4)), 5, vocab=v_one)
+    def pass_on(j, k):
+        if k > 0:
+
+            @pl.when(is_outer == 0)
+            def _():
+                relay_landed(j, k - 1)
+                relay(j, k - 1).start()
+
+        landed(j, k)
+        forward(j, k).start()
+
+    for what, j in service_order(plan, n_tiles):
+        if what == "h line":
+            arrived(h_place(v, z_one), 1, hid=z_one)
+            arrived(h_place(v, lax.rem(z_one + 2, 4)), 2, hid=z_one)
+            h_own.wait()
+            h_chip.start()
+            h_core.start()
+        elif what == "h chip":
+            arrived(h_place(v_two), 3, vocab=v_two)
+            h_both.start()
         else:
-            complete(j - 1)
-            compute(j - 1)
-        if j + 2 < n_chunks:
-            own(j + 2).start()
+            pass_on(j, what)
+            if what == 2 and j == 0:
+                arrived(h_place(v_one), 4, vocab=v_one)
+                arrived(h_place(lax.rem(v_one + 2, 4)), 5, vocab=v_one)
+            elif what == 2:
+                complete(j - 1)
+                compute(j - 1)
+            if what == 2 and j + 2 < n_chunks:
+                own(j + 2).start()
     complete(n_chunks - 1)
     compute(n_chunks - 1)
 
@@ -275,6 +305,13 @@
         send_outer(j).wait_send()
         for k in range(3):
             forward(j, k).wait_send()
+
+    @pl.when(is_outer == 0)
+    def _():
+        for j in range(n_chunks):
+            for s in range(2):
+                relay(j, s).wait_send()
+
     for copy in (h_two, h_one, h_relay, h_chip, h_core, h_both):
         copy.wait_send()
 
@@ -343,15 +380,34 @@
         v_send(d).wait_send()
 
 
-def finish_kernel(c_ref, scale_ref, off_ref, tgt_ref, out_ref, tgt_out_ref):
-    n, n_cols = out_ref.shape
-    at = pl.ds(pl.multiple_of(pl.program_id(0) * n, n), n)
-    for start in range(0, n_cols, TILE):
-        t, stop = start // TILE, min(n_cols, start + TILE)
-        out_ref[:, start:stop] = (
-            c_ref[at, start:stop] * scale_ref[at, t : t + 1] + off_ref[at, t : t + 1]
-        )
+def finish_kernel(c_ref, scale_ref, off_ref, tgt_ref, out_ref, tgt_out_ref, buf, sems):
+    slots, n, n_cols = buf.shape
+    steps = c_ref.shape[0] // n
+
+    def put(i):
+        slot = lax.rem(i, slots)
+        at = pl.ds(pl.multiple_of(i * n, n), n)
+        return pltpu.make_async_copy(buf.at[slot], out_ref.at[at], sems.at[slot])
+
+    @pl.loop(0, steps)
+    def _(i):
+        slot = lax.rem(i, slots)
+        at = pl.ds(pl.multiple_of(i * n, n), n)
+
+        @pl.when(i >= slots)
+        def _():
+            put(i - slots).wait()
+
+        for start in range(0, n_cols, TILE):
+            t, stop = start // TILE, min(n_cols, start + TILE)
+            buf[slot, :, start:stop] = (
+                c_ref[at, start:stop] * scale_ref[at, t : t + 1] + off_ref[at, t : t + 1]
+            )
+        put(i).start()
+
     tgt_out_ref[...] = tgt_ref[...]
+    for i in range(max(0, steps - slots), steps):
+        put(i).wait()
 
 
 def solution(mesh):
@@ -369,16 +425,17 @@
         hbm = pl.BlockSpec(memory_space=pltpu.HBM)
         dma = pltpu.SemaphoreType.DMA
         table = pltpu.VMEM((rows, LANES), F32)
-        c, scale, off, tgt = pl.pallas_call(
+        c, scale, off, tgt, _ = pl.pallas_call(
             functools.partial(prefix_kernel, n_cols),
             out_shape=(
                 pltpu.VMEM((rows, n_cols), F32),
                 pltpu.VMEM((rows, LANES), F32),
                 pltpu.VMEM((rows, LANES), F32),
                 pltpu.VMEM((1, rows), F32),
+                jax.ShapeDtypeStruct((2, depth // 2, n_cols), BF16),
             ),
             in_specs=[hbm, hbm, vmem, vmem],
-            out_specs=[vmem] * 4,
+            out_specs=[vmem] * 4 + [hbm],
             scratch_shapes=[
                 pltpu.VMEM((4 * depth, n_cols), BF16),
                 pltpu.VMEM((rows, 4 * depth), BF16),
@@ -396,6 +453,8 @@
                 dma((n_chunks, 3)),
                 dma((n_chunks, 3)),
                 dma((n_chunks, 3)),
+                dma((n_chunks, 2)),
+                dma((n_chunks, 2)),
                 dma((n_chunks,)),
                 dma,
                 dma((6,)),
@@ -410,19 +469,16 @@
             ),
             name="prefix",
         )(h_blk, w_blk, temp_blk.reshape(1, rows), tgt_blk.reshape(1, rows))
-        n = min(rows, 128)
+        n = min(rows, 64)
         cdf, cdf_tgt = pl.pallas_call(
             finish_kernel,
-            grid=(rows // n,),
             out_shape=(
                 jax.ShapeDtypeStruct((rows, n_cols), F32),
                 jax.ShapeDtypeStruct((1, rows), F32),
             ),
             in_specs=[vmem] * 4,
-            out_specs=[
-                pl.BlockSpec((n, n_cols), lambda i: (i, 0)),
-                pl.BlockSpec((1, rows), lambda i: (0, 0)),
-            ],
+            out_specs=[hbm, vmem],
+            scratch_shapes=[pltpu.VMEM((4, n, n_cols), F32), dma((4,))],
             compiler_params=pltpu.CompilerParams(vmem_limit_bytes=9 << 20),
             name="finish",
         )(c, scale, off, tgt)

time: 353 us -> 412 us (1.17)
  Pallas kernels: 352 us -> 411 us
    pallas_call x1, Pallas kernels: 341 us -> 401 us  [local_step(): pl.pallas_call(functools.partial(prefix_kernel, n_cols), out_shape=(pltpu...]
where the time goes in v3:
time: 412 us
  Pallas kernels  411 us (100%)
    pallas_call x1, Pallas kernels, local_step(): pl.pallas_call(functools.partial(prefix_kernel, n_cols), out_shape=(pltpu...  401 us
    pallas_call x1, Pallas kernels, local_step(): pl.pallas_call(finish_kernel, out_shape=(jax.ShapeDtypeStruct((rows, n_co...  10.3 us

profile of v3, /device:TPU:0, one launch (start us, length us, event | category | flops | bytes accessed | tf_op | source)
XLA Modules:
  0.0 412.2 jit_solution(14993077224180146434)
XLA Ops:
  0.6 401.1 %prefix.1 = (f32[1024,6272]{1,0:T(8,128)S(1)}, f32[1024,128]{1,0:T(8,128)S(1)}, f32[1024,128]{1,0:T(8,128)S(1)}, f32[1,1024]{1,0:T(1,128)S(1)}, bf16[2,256,6272]{2,1,0:T(8,128)(2,1)}) custom-call(bf16[1024,512]{1,0:T(8,128)(2,1)} %h_ref.1, bf16[512,25088]{1,0:T(8,128)(2,1)} %w_ref.1, f32[1,1024]{1,0:T(1,128)} %bitcast.3, s32[1,1024]{1,0:T(1,128)} %bitcast.4), custom_call_target="tpu_custom_call" | custom-call | tf_op jit(solution)/shard_map/prefix/pallas_call | solution.py:428
  401.8 10.3 %finish.1 = (f32[1024,6272]{1,0:T(8,128)}, f32[1,1024]{1,0:T(1,128)}) custom-call(f32[1024,6272]{1,0:T(8,128)S(1)} %get-tuple-element.8.c_ref, f32[1024,128]{1,0:T(8,128)S(1)} %get-tuple-element.9.scale_ref, f32[1024,128]{1,0:T(8,128)S(1)} %get-tuple-element.10.off_ref, f32[1,1024]{1,0:T(1,128)S(1)} %get-tuple-element.11.tgt_ref), custom_call_target="tpu_custom_call" | custom-call | tf_op jit(solution)/shard_map/finish/pallas_call | solution.py:473
